TPU v7x, 32 devices: a whole 2x2x4 slice. The times are simulated.
32 devices in a mesh: dp: 4 (over z), mp: 8 (over y, x, core).
Axes of the slice: x: 2, y: 2, z: 4, core: 2. Of those that a mesh axis runs over, the one named last changes fastest.
Arguments:
- tokens: bfloat16 [4096, 4096], P('dp', 'mp'), may hold values from -6 to 6
- decay: float32 [4096, 16], P('dp'), may hold values from 0.75 to 1, as said below
- state: float32 [128, 256, 8192], P('dp', None, 'mp'), may hold values from -24 to 24
- w_query: bfloat16 [4096, 4096], P(None, 'mp'), may hold values from -0.09375 to 0.09375
- w_key: bfloat16 [4096, 4096], P(None, 'mp'), may hold values from -0.09375 to 0.09375
- w_value: bfloat16 [4096, 8192], P(None, 'mp'), may hold values from -0.09375 to 0.09375
- w_gate: bfloat16 [4096, 8192], P(None, 'mp'), may hold values from -0.09375 to 0.09375
- w_out: bfloat16 [8192, 4096], P('mp'), may hold values from -0.09375 to 0.09375
- norm_gain: float32 [8192], P('mp'), may hold values from 0.25 to 1.75
Outputs:
- layer_out: bfloat16 [4096, 4096], P('dp', 'mp')
- new_state: float32 [128, 256, 8192], P('dp', None, 'mp')
Inputs may be any that keep to these rules, and one draw needn't show every extreme that they name: `decay`: each head has its own base rate over all tokens, varied somewhat from token to token.
All inputs are finite; a program needn't handle non-finite values.
Results may differ from a plain program's by a relative error of at most 0.0071.
Values may be sent and summed in bfloat16 or wider, within the bound.
A program may use at most 256 MiB of HBM per device.

v0:
```python
import jax
import jax.numpy as jnp
from jax import lax
from jax.sharding import PartitionSpec as P

HEAD = 256
VHEAD = 512
NEW = 32
EPS = 0.1


def partner(shard, axis, bit):
    return lax.ppermute(shard, axis, [(i, i ^ 1 << bit) for i in range(lax.axis_size(axis))])


def per_device(tokens, decay, state, w_query, w_key, w_value, w_gate, w_out, norm_gain):
    highest = lax.Precision.HIGHEST
    tok_rows = tokens.shape[0]
    qk_columns = w_query.shape[1]
    v_columns = w_value.shape[1]
    head_span = max(1, HEAD // qk_columns)
    groups = max(1, qk_columns // HEAD)
    qk_width = qk_columns // groups
    v_width = v_columns // groups
    sequences = tok_rows // NEW
    bit_count = head_span.bit_length() - 1
    device_index = lax.axis_index("mp")
    first_head = device_index * qk_columns // HEAD
    qk_zeros = jnp.zeros((tok_rows, qk_columns), jnp.float32)
    v_zeros = jnp.zeros((tok_rows, v_columns), jnp.float32)
    carried = (qk_zeros, qk_zeros, v_zeros, v_zeros)
    segment = lax.all_gather(tokens, "mp", axis=1, tiled=True)
    updated = []
    for running, weight in zip(carried, (w_query, w_key, w_value, w_gate)):
        updated.append(jnp.dot(segment, weight, preferred_element_type=jnp.float32))
    query, key_proj, value_proj, gate_proj = tuple(updated)
    query = (query * HEAD ** (-0.5)).astype(jnp.bfloat16).reshape(tok_rows, groups, qk_width)
    key_proj = key_proj.astype(jnp.bfloat16).reshape(tok_rows, groups, qk_width)
    value_proj = value_proj.astype(jnp.bfloat16)
    for bit_number in range(bit_count):
        other_query, other_key = partner((query, key_proj), "mp", bit_number)
        upper_half = device_index >> bit_number & 1 == 1
        query = jnp.where(
            upper_half,
            jnp.concatenate([other_query, query], 2),
            jnp.concatenate([query, other_query], 2),
        )
        key_proj = jnp.where(
            upper_half,
            jnp.concatenate([other_key, key_proj], 2),
            jnp.concatenate([key_proj, other_key], 2),
        )
    query_block = query.reshape(sequences, NEW, groups, HEAD)
    key_block = key_proj.reshape(sequences, NEW, groups, HEAD)
    value_block = value_proj.reshape(sequences, NEW, groups, v_width)
    decay_rates = lax.dynamic_slice_in_dim(decay, first_head, groups, 1).reshape(
        sequences, NEW, groups
    )
    log_cumul = jnp.cumsum(jnp.log(decay_rates), axis=1)
    old_state = state.reshape(sequences, HEAD, groups, v_width)
    from_state = jnp.einsum(
        "bngk,bkgv->bngv", query_block.astype(jnp.float32), old_state, precision=highest
    )
    scores = jnp.einsum(
        "bngk,bmgk->bgnm", query_block, key_block, preferred_element_type=jnp.float32
    )
    along = jnp.transpose(log_cumul, (0, 2, 1))
    log_gap = along[:, :, :, None] - along[:, :, None, :]
    causal = jnp.arange(NEW)[:, None] >= jnp.arange(NEW)[None, :]
    factor = jnp.where(causal, jnp.exp(jnp.where(causal, log_gap, 0.0)), 0.0)
    weights = (scores * factor).astype(jnp.bfloat16)
    in_block = jnp.einsum(
        "bgnm,bmgv->bngv", weights, value_block, preferred_element_type=jnp.float32
    )
    retained = jnp.exp(log_cumul)[..., None] * from_state + in_block
    final_log = log_cumul[:, -1, :]
    carry_scale = jnp.exp(final_log[:, None, :] - log_cumul)
    decayed_keys = key_block.astype(jnp.float32) * carry_scale[..., None]
    fresh = jnp.einsum(
        "bngk,bngv->bkgv", decayed_keys, value_block.astype(jnp.float32), precision=highest
    )
    new_state = jnp.exp(final_log)[:, None, :, None] * old_state + fresh
    new_state = new_state.reshape(sequences, HEAD, v_columns)
    retained = retained.reshape(tok_rows, groups, v_width)
    running = jnp.sum(retained, axis=-1)
    squares = jnp.sum(retained * retained, axis=-1)
    for bit_number in range(bit_count):
        other_sum, other_square = partner((running, squares), "mp", bit_number)
        running = running + other_sum
        squares = squares + other_square
    centre = running / VHEAD
    variance = squares / VHEAD - centre * centre
    deviation = retained - centre[..., None]
    normed = deviation * lax.rsqrt(variance + EPS)[..., None]
    gated_out = (normed.reshape(tok_rows, v_columns) * norm_gain * jax.nn.silu(gate_proj)).astype(
        jnp.bfloat16
    )
    partial_terms = jnp.dot(gated_out, w_out, preferred_element_type=jnp.float32)
    layer_out = lax.psum_scatter(partial_terms, "mp", scatter_dimension=1, tiled=True).astype(
        jnp.bfloat16
    )
    return (layer_out, new_state)


def solution(mesh):
    placed = (
        P("dp", "mp"),
        P("dp", None),
        P("dp", None, "mp"),
        P(None, "mp"),
        P(None, "mp"),
        P(None, "mp"),
        P(None, "mp"),
        P("mp", None),
        P("mp"),
    )
    return jax.shard_map(
        per_device,
        mesh=mesh,
        in_specs=placed,
        out_specs=(P("dp", "mp"), P("dp", None, "mp")),
        check_vma=False,
    )
```

profile of v0, /device:TPU:0, one launch (start us, length us, event | category | flops | bytes accessed | tf_op | source)
XLA Modules:
  0.0 312.2 jit_solution(14913403613981106068)
XLA Ops:
  9.5 2.0 fusion.33
  11.8 33.6 %copy.84 = f32[32,256,1024]{1,2,0:T(8,128)} copy(f32[32,256,1024]{2,1,0:T(8,128)} %param.11) | data formatting | bytes 67108864 | tf_op args[2]
  47.5 20.9 %all-gather.2.cloned.1.call-done = bf16[1024,4096]{1,0:T(8,128)(2,1)} async-done(((bf16[1024,512]{1,0:T(8,128)(2,1)}), bf16[1024,4096]{1,0:T(8,128)(2,1)}) %all-gather.2.cloned.1.call-update) | async-done | bytes 8388624 | tf_op jit(solution)/shard_map/all_gather | solution.py:32
  68.5 14.7 %convolution_convert_fusion = bf16[1024,1024]{1,0:T(8,128)(2,1)} fusion(bf16[1024,4096]{1,0:T(8,128)(2,1)} %all-gather.2.cloned.1.call-done, bf16[4096,1024]{1,0:T(8,128)(2,1)} %param.14), kind=kOutput, calls=%fused_computation.11 | convolution fusion | flops 8590983168 | bytes 18874368 | tf_op jit(solution)/shard_map/dot_general | solution.py:35
  83.1 3.3 %reshape.64 = bf16[32,32,2,512]{3,2,1,0:T(2,128)(2,1)S(1)} reshape(bf16[1024,1024]{1,0:T(8,128)(2,1)} %convolution_convert_fusion) | data formatting | bytes 4194304 | tf_op jit(solution)/shard_map/reshape | solution.py:55
  86.5 10.0 %convolution_convert_fusion.1 = bf16[1024,512]{1,0:T(8,128)(2,1)} fusion(bf16[1024,4096]{1,0:T(8,128)(2,1)} %all-gather.2.cloned.1.call-done, bf16[4096,512]{1,0:T(8,128)(2,1)} %param.13), kind=kOutput, calls=%fused_computation.14 | convolution fusion | flops 4295491584 | bytes 13631488 | tf_op jit(solution)/shard_map/dot_general | solution.py:35
  96.5 1.3 reshape_reshape.7
  97.8 10.0 %multiply_convert_fusion.2 = bf16[1024,512]{1,0:T(8,128)(2,1)} fusion(bf16[1024,4096]{1,0:T(8,128)(2,1)} %all-gather.2.cloned.1.call-done, bf16[4096,512]{1,0:T(8,128)(2,1)} %param.12), kind=kOutput, calls=%fused_computation.10 | convolution fusion | flops 4296015872 | bytes 13631488 | tf_op jit(solution)/shard_map/dot_general | solution.py:35
  107.9 2.2 reshape_reshape.6
  110.1 21.4 %fusion.18 = f32[32,2,32,512]{3,2,1,0:T(8,128)} fusion(f32[32,256,2,512]{1,3,2,0:T(8,128)} %bitcast.37, bf16[32,32,2,256]{3,2,1,0:T(2,128)(2,1)} %reshape_reshape.6), kind=kOutput, calls=%fused_computation.25 | convolution fusion | flops 3221225472 | bytes 38797312 | tf_op jit(solution)/shard_map/bngk,bkgv->bngv/dot_general | solution.py:61
  131.5 4.9 %fusion.26 = (f32[32,32,2]{1,2,0:T(2,128)S(1)}, f32[32,32,2]{1,2,0:T(2,128)S(1)}, f32[32,32,2,512]{3,1,2,0:T(8,128)}) fusion(bf16[32,32,2,512]{3,2,1,0:T(2,128)(2,1)S(1)} %reshape.64, bf16[32,32,2,256]{3,2,1,0:T(2,128)(2,1)S(1)} %reshape_reshape.7, bf16[32,32,2,256]{3,2,1,0:T(2,128)(2,1)} %reshape_reshape.6, f32[32,2,32]{2,1,0:T(2,128)S(1)} %copy.89, ...), kind=kOutput, calls=%fused_computation.40 | convolution fusion | flops 106229760 | bytes 12616704 | tf_op jit(solution)/shard_map/bgnm,bmgv->bngv/dot_general | solution.py:72
  136.6 1.0 copy.94
  138.7 2.9 mul.81
  141.6 3.0 copy.107
  144.6 3.3 %copy.92 = f32[32,32,2,512]{3,2,1,0:T(2,128)S(1)} copy(f32[32,32,2,512]{3,1,2,0:T(8,128)S(1)} %copy-done) | data formatting | bytes 8388608 | tf_op jit(solution)/shard_map/add | solution.py:75
  147.9 3.0 copy.105
  150.9 1.4 sub.51
  152.3 2.9 copy.106
  155.2 31.2 %fusion = f32[1024,4096]{1,0:T(8,128)} fusion(bf16[1024,4096]{1,0:T(8,128)(2,1)} %param.16, f32[1024,1024]{1,0:T(8,128)} %bitcast.44, f32[1024,1024]{1,0:T(8,128)} %bitcast.45, f32[1024,1024]{1,0:T(8,128)} %bitcast.46, f32[1024]{0:T(1024)S(1)} %copy-done.4, bf16[1024,4096]{1,0:T(8,128)(2,1)} %all-gather.2.cloned.1.call-done, bf16[4096,1024]{1,0:T(8,128)(2,1)} %param.15), kind=kOutput, calls=%fused_computation.5 | convolution fusion | flops 17189306368 | bytes 54530048 | tf_op jit(solution)/shard_map/dot_general | solution.py:98
  187.2 1.4 copy.101
  188.6 28.9 %bitcast_add_fusion = f32[32,256,2,512]{1,3,2,0:T(8,128)} fusion(f32[32,256,2,512]{1,3,2,0:T(8,128)} %bitcast.38, f32[32,2]{1,0:T(8,128)S(1)} %copy.98, bf16[32,32,2,512]{3,2,1,0:T(2,128)(2,1)S(1)} %reshape.64, f32[32,32,2]{1,2,0:T(2,128)S(1)} %copy.101, bf16[32,32,2,256]{3,2,1,0:T(2,128)(2,1)S(1)} %reshape_reshape.7), kind=kOutput, calls=%fused_computation | convolution fusion | flops 3239051264 | bytes 70263040 | tf_op jit(solution)/shard_map/bngk,bngv->bkgv/dot_general | solution.py:79
  217.5 33.7 %copy.103 = f32[32,256,1024]{2,1,0:T(8,128)} copy(f32[32,256,1024]{1,2,0:T(8,128)} %bitcast.39) | data formatting | bytes 67108864
  251.3 51.4 %reduce-scatter.2.cloned.1.call-done = f32[1024,512]{1,0:T(8,128)} async-done(((f32[1024,4096]{1,0:T(8,128)}), f32[1024,512]{1,0:T(8,128)}) %reduce-scatter.2.cloned.1.call-update) | async-done | bytes 2097168 | tf_op jit(solution)/shard_map/reduce_scatter | solution.py:99
  302.7 2.7 convert_element_type.28
  (31 shorter events, 6.6 us)
Async XLA Ops:
  7.2 61.3 %all-gather.2.cloned.1.call-start = ((), (), s32[]{:S(2)}) async-start(), calls=%async_computation.1 | async-start | bytes 9437184 | tf_op jit(solution)/shard_map/all_gather | solution.py:32
  7.9 294.8 %reduce-scatter.2.cloned.1.call-start = ((), (), s32[]{:S(2)}) async-start(), calls=%async_computation.2 | async-start | bytes 18874368 | tf_op jit(solution)/shard_map/reduce_scatter | solution.py:99
  45.6 0.6 copy-start.2
  141.6 3.0 copy-start
  147.9 3.0 copy-start.1
  152.3 3.0 copy-start.4
  186.5 0.7 copy-start.3
Sparse Core Ops, SparseCore 0:
  9.8 58.5 all-gather.1
  186.6 115.9 reduce-scatter.1
where the time goes:
time: 314 us; the launch traced here: 312 us
  matrix products  121 us (39%)
  local copies, waits for them, and re-layouts  98 us (31%)
  waiting for transfers between devices  73 us (23%)
  between operations  14.2 us (5%)
  other arithmetic  5.65 us (2%)
    unnamed x15, local copies, waits for them, and re-layouts  77.5 us
    reduce_scatter x1, waiting for transfers between devices, per_device(): lax.psum_scatter(partial_terms, 'mp', scatter_dimension=1, tiled=True)  51.4 us
    dot_general x3, matrix products, per_device(): updated.append(jnp.dot(segment, weight, preferred_element_type=jnp.float32))  34.7 us
    dot_general x1, matrix products, per_device(): jnp.dot(gated_out, w_out, preferred_element_type=jnp.float32)  31.2 us
    dot_general x1, matrix products, per_device(): jnp.einsum('bngk,bngv->bkgv', decayed_keys, value_block.astype(jnp.float3...  28.9 us
    dot_general x1, matrix products, per_device(): jnp.einsum('bngk,bkgv->bngv', query_block.astype(jnp.float32), old_state,...  21.4 us
    all_gather x1, waiting for transfers between devices, per_device(): segment = lax.all_gather(tokens, 'mp', axis=1, tiled=True)  20.9 us
  transfers between devices with their start and end apart: 2, of which 2 were waited for; matrix products, arithmetic and copies ran while one was open for 33% of the time, Pallas kernels for 0%

commit v1 on v0

--- a/solution.py
+++ b/solution.py
@@ -29,7 +29,8 @@
     qk_zeros = jnp.zeros((tok_rows, qk_columns), jnp.float32)
     v_zeros = jnp.zeros((tok_rows, v_columns), jnp.float32)
     carried = (qk_zeros, qk_zeros, v_zeros, v_zeros)
-    segment = lax.all_gather(tokens, "mp", axis=1, tiled=True)
+    last = lax.all_gather(tokens, "mp")
+    segment = jnp.concatenate(last, axis=1)
     updated = []
     for running, weight in zip(carried, (w_query, w_key, w_value, w_gate)):
         updated.append(jnp.dot(segment, weight, preferred_element_type=jnp.float32))

time: 314 us -> 324 us (1.032)
  local copies, waits for them, and re-layouts: 98 us -> 110 us
    reshape x0 -> x1, local copies, waits for them, and re-layouts: none -> 11.5 us  [per_device(): segment = jnp.concatenate(last, axis=1)]
  transfers between devices with their start and end apart: 2 -> 2, of which waited for: 2 -> 2; matrix products, arithmetic and copies ran while one was open for 33% -> 32% of each run, Pallas kernels for 0% -> 0%
where the time goes in v1:
time: 324 us; the launch traced here: 323 us
  matrix products  122 us (38%)
  local copies, waits for them, and re-layouts  110 us (34%)
  waiting for transfers between devices  71.5 us (22%)
  between operations  14.2 us (4%)
  other arithmetic  5.65 us (2%)
    unnamed x15, local copies, waits for them, and re-layouts  77.4 us
    reduce_scatter x1, waiting for transfers between devices, per_device(): lax.psum_scatter(partial_terms, 'mp', scatter_dimension=1, tiled=True)  51.4 us
    dot_general x3, matrix products, per_device(): updated.append(jnp.dot(segment, weight, preferred_element_type=jnp.float32))  34.9 us
    dot_general x1, matrix products, per_device(): jnp.dot(gated_out, w_out, preferred_element_type=jnp.float32)  31.4 us
    dot_general x1, matrix products, per_device(): jnp.einsum('bngk,bngv->bkgv', decayed_keys, value_block.astype(jnp.float3...  28.9 us
    dot_general x1, matrix products, per_device(): jnp.einsum('bngk,bkgv->bngv', query_block.astype(jnp.float32), old_state,...  21.5 us
    all_gather x1, waiting for transfers between devices, per_device(): last = lax.all_gather(tokens, 'mp')  19.4 us
    reshape x1, local copies, waits for them, and re-layouts, per_device(): segment = jnp.concatenate(last, axis=1)  11.5 us
  transfers between devices with their start and end apart: 2, of which 2 were waited for; matrix products, arithmetic and copies ran while one was open for 32% of the time, Pallas kernels for 0%

profile of v1, /device:TPU:0, one launch (start us, length us, event | category | flops | bytes accessed | tf_op | source)
XLA Modules:
  0.0 322.8 jit_solution(16683079162742021138)
XLA Ops:
  9.5 2.0 fusion.33
  11.8 33.6 %copy.106 = f32[32,256,1024]{1,2,0:T(8,128)} copy(f32[32,256,1024]{2,1,0:T(8,128)} %param.11) | data formatting | bytes 67108864 | tf_op args[2]
  47.5 19.4 %all-gather.3.cloned.1.call-done = bf16[8192,512]{1,0:T(8,128)(2,1)} async-done(((bf16[1024,512]{1,0:T(8,128)(2,1)}), bf16[8192,512]{1,0:T(8,128)(2,1)}) %all-gather.3.cloned.1.call-update) | async-done | bytes 8388624 | tf_op jit(solution)/shard_map/all_gather | solution.py:32
  66.9 11.5 %copy.105 = bf16[1024,8,512]{0,2,1:T(8,128)(2,1)} copy(bf16[1024,8,512]{2,0,1:T(8,128)(2,1)} %bitcast.54) | data formatting | bytes 16777216 | tf_op jit(solution)/shard_map/reshape | solution.py:33
  78.4 14.7 %convolution_convert_fusion = bf16[1024,1024]{1,0:T(8,128)(2,1)} fusion(bf16[1024,4096]{0,1:T(8,128)(2,1)} %bitcast.44, bf16[4096,1024]{1,0:T(8,128)(2,1)} %param.14), kind=kOutput, calls=%fused_computation.11 | convolution fusion | flops 8590983168 | bytes 18874368 | tf_op jit(solution)/shard_map/dot_general | solution.py:36
  93.1 3.3 %reshape.72 = bf16[32,32,2,512]{3,2,1,0:T(2,128)(2,1)S(1)} reshape(bf16[1024,1024]{1,0:T(8,128)(2,1)} %convolution_convert_fusion) | data formatting | bytes 4194304 | tf_op jit(solution)/shard_map/reshape | solution.py:56
  96.4 10.1 %convolution_convert_fusion.1 = bf16[1024,512]{1,0:T(8,128)(2,1)} fusion(bf16[1024,4096]{0,1:T(8,128)(2,1)} %bitcast.45, bf16[4096,512]{1,0:T(8,128)(2,1)} %param.13), kind=kOutput, calls=%fused_computation.14 | convolution fusion | flops 4295491584 | bytes 13631488 | tf_op jit(solution)/shard_map/dot_general | solution.py:36
  106.5 1.5 reshape_reshape.7
  108.0 10.1 %multiply_convert_fusion.2 = bf16[1024,512]{1,0:T(8,128)(2,1)} fusion(bf16[1024,4096]{0,1:T(8,128)(2,1)} %bitcast.46, bf16[4096,512]{1,0:T(8,128)(2,1)} %param.12), kind=kOutput, calls=%fused_computation.10 | convolution fusion | flops 4296015872 | bytes 13631488 | tf_op jit(solution)/shard_map/dot_general | solution.py:36
  118.1 2.2 reshape_reshape.6
  120.3 21.5 %fusion.18 = f32[32,2,32,512]{3,2,1,0:T(8,128)} fusion(f32[32,256,2,512]{1,3,2,0:T(8,128)} %bitcast.41, bf16[32,32,2,256]{3,2,1,0:T(2,128)(2,1)} %reshape_reshape.6), kind=kOutput, calls=%fused_computation.25 | convolution fusion | flops 3221225472 | bytes 38797312 | tf_op jit(solution)/shard_map/bngk,bkgv->bngv/dot_general | solution.py:62
  141.8 4.9 %fusion.26 = (f32[32,32,2]{1,2,0:T(2,128)S(1)}, f32[32,32,2]{1,2,0:T(2,128)S(1)}, f32[32,32,2,512]{3,1,2,0:T(8,128)}) fusion(bf16[32,32,2,512]{3,2,1,0:T(2,128)(2,1)S(1)} %reshape.72, bf16[32,32,2,256]{3,2,1,0:T(2,128)(2,1)S(1)} %reshape_reshape.7, bf16[32,32,2,256]{3,2,1,0:T(2,128)(2,1)} %reshape_reshape.6, f32[32,2,32]{2,1,0:T(2,128)S(1)} %copy.111, ...), kind=kOutput, calls=%fused_computation.40 | convolution fusion | flops 106229760 | bytes 12616704 | tf_op jit(solution)/shard_map/bgnm,bmgv->bngv/dot_general | solution.py:73
  148.9 3.1 mul.81
  152.0 3.0 copy.129
  155.0 3.3 %copy.114 = f32[32,32,2,512]{3,2,1,0:T(2,128)S(1)} copy(f32[32,32,2,512]{3,1,2,0:T(8,128)S(1)} %copy-done.1) | data formatting | bytes 8388608 | tf_op jit(solution)/shard_map/add | solution.py:76
  158.4 3.0 copy.127
  161.3 1.4 sub.51
  162.7 2.9 copy.128
  165.7 31.4 %fusion = f32[1024,4096]{1,0:T(8,128)} fusion(bf16[1024,4096]{1,0:T(8,128)(2,1)} %param.16, f32[1024,1024]{1,0:T(8,128)} %bitcast.48, f32[1024,1024]{1,0:T(8,128)} %bitcast.49, f32[1024,1024]{1,0:T(8,128)} %bitcast.50, f32[1024]{0:T(1024)S(1)} %copy-done, bf16[1024,4096]{0,1:T(8,128)(2,1)} %bitcast.47, bf16[4096,1024]{1,0:T(8,128)(2,1)} %param.15), kind=kOutput, calls=%fused_computation.5 | convolution fusion | flops 17189306368 | bytes 54530048 | tf_op jit(solution)/shard_map/dot_general | solution.py:99
  197.8 1.4 copy.123
  199.2 28.9 %bitcast_add_fusion = f32[32,256,2,512]{1,3,2,0:T(8,128)} fusion(f32[32,256,2,512]{1,3,2,0:T(8,128)} %bitcast.42, f32[32,2]{1,0:T(8,128)S(1)} %copy.120, bf16[32,32,2,512]{3,2,1,0:T(2,128)(2,1)S(1)} %reshape.72, f32[32,32,2]{1,2,0:T(2,128)S(1)} %copy.123, bf16[32,32,2,256]{3,2,1,0:T(2,128)(2,1)S(1)} %reshape_reshape.7), kind=kOutput, calls=%fused_computation | convolution fusion | flops 3239051264 | bytes 70263040 | tf_op jit(solution)/shard_map/bngk,bngv->bkgv/dot_general | solution.py:80
  228.1 33.7 %copy.125 = f32[32,256,1024]{2,1,0:T(8,128)} copy(f32[32,256,1024]{1,2,0:T(8,128)} %bitcast.43) | data formatting | bytes 67108864
  261.8 51.4 %reduce-scatter.2.cloned.1.call-done = f32[1024,512]{1,0:T(8,128)} async-done(((f32[1024,4096]{1,0:T(8,128)}), f32[1024,512]{1,0:T(8,128)}) %reduce-scatter.2.cloned.1.call-update) | async-done | bytes 2097168 | tf_op jit(solution)/shard_map/reduce_scatter | solution.py:100
  313.3 2.7 convert_element_type.28
  (32 shorter events, 7.7 us)
Async XLA Ops:
  7.2 59.7 %all-gather.3.cloned.1.call-start = ((), (), s32[]{:S(2)}) async-start(), calls=%async_computation.2 | async-start | bytes 9437184 | tf_op jit(solution)/shard_map/all_gather | solution.py:32
  7.9 305.4 %reduce-scatter.2.cloned.1.call-start = ((), (), s32[]{:S(2)}) async-start(), calls=%async_computation.1 | async-start | bytes 18874368 | tf_op jit(solution)/shard_map/reduce_scatter | solution.py:100
  45.5 0.6 copy-start.3
  152.0 3.0 copy-start.1
  158.4 3.0 copy-start.2
  162.7 3.0 copy-start
  197.1 0.7 copy-start.4
Sparse Core Ops, SparseCore 0:
  9.9 56.9 all-gather.2
  197.2 115.9 reduce-scatter.1
